TPU v7x, 32 devices: a whole 2x2x4 slice. The times are simulated.
32 devices in a mesh: rep: 4 (over y, x), fsdp: 8 (over z, core).
Axes of the slice: x: 2, y: 2, z: 4, core: 2. Of those that a mesh axis runs over, the one named last changes fastest.
Arguments:
- inputs: bfloat16 [32, 1024, 768], P(('rep', 'fsdp')), may hold values from -6 to 6
- w_query: bfloat16 [768, 768], P('fsdp'), may hold values from -0.21875 to 0.21875
- w_key: bfloat16 [768, 768], P('fsdp'), may hold values from -0.21875 to 0.21875
- w_value: bfloat16 [768, 768], P('fsdp'), may hold values from -0.21875 to 0.21875
- w_out: bfloat16 [768, 768], P('fsdp'), may hold values from -0.875 to 0.875
- w_gate: bfloat16 [768, 2048], P('fsdp'), may hold values from -0.21875 to 0.21875
- w_up: bfloat16 [768, 2048], P('fsdp'), may hold values from -0.21875 to 0.21875
- w_down: bfloat16 [2048, 768], P('fsdp'), may hold values from -0.125 to 0.125
- norm_attn: bfloat16 [768], P('fsdp'), may hold values from 0.25 to 1.75
- norm_ffn: bfloat16 [768], P('fsdp'), may hold values from 0.25 to 1.75
- lengths: int32 [32], P(('rep', 'fsdp')), may hold values from 64 to 1024, as said below
- cotangent: bfloat16 [32, 1024, 768], P(('rep', 'fsdp')), may hold values from -6 to 6
Outputs:
- output: bfloat16 [32, 1024, 768], P(('rep', 'fsdp'))
- grad_input: bfloat16 [32, 1024, 768], P(('rep', 'fsdp'))
- grad_query: float32 [768, 768], P('fsdp')
- grad_key: float32 [768, 768], P('fsdp')
- grad_value: float32 [768, 768], P('fsdp')
- grad_out: float32 [768, 768], P('fsdp')
- grad_gate: float32 [768, 2048], P('fsdp')
- grad_up: float32 [768, 2048], P('fsdp')
- grad_down: float32 [2048, 768], P('fsdp')
- grad_norm_attn: float32 [768], P('fsdp')
- grad_norm_ffn: float32 [768], P('fsdp')
Inputs may be any that keep to these rules, and one draw needn't show every extreme that they name: Tokens at positions lengths[s] and beyond are padding. Some sequence has exactly 1024 valid tokens.
All inputs are finite; a program needn't handle non-finite values.
Results may differ from a plain program's by a relative error of at most 0.018.
Values may be sent and summed in bfloat16 or wider, within the bound.
No kernel may reach another device: no remote copies, remote signals or barrier semaphores. Data moves between devices by JAX's collectives and lax.ppermute only.
A program may use at most 192 MiB of HBM per device.

v0:
```python
import jax
import jax.numpy as jnp
from jax import lax
from jax.sharding import PartitionSpec as P

HEADS = 12
EPSILON = 1e-05


def rotary_tables(seq_length, head_width):
    half_width = head_width // 2
    position = jnp.arange(seq_length, dtype=jnp.float32)
    inverse = 10000.0 ** (-(jnp.arange(half_width, dtype=jnp.float32) * 2.0 / head_width))
    angles = position[:, None] * inverse[None, :]
    return (jnp.cos(angles)[:, None, :], jnp.sin(angles)[:, None, :])


def rotate(values, cosine, sine_table):
    half_width = values.shape[-1] // 2
    former = values[..., :half_width]
    latter = values[..., half_width:]
    return jnp.concatenate(
        [former * cosine - latter * sine_table, latter * cosine + former * sine_table], axis=-1
    )


def unrotate(grads_in, cosine, sine_table):
    half_width = grads_in.shape[-1] // 2
    former = grads_in[..., :half_width]
    latter = grads_in[..., half_width:]
    return jnp.concatenate(
        [former * cosine + latter * sine_table, latter * cosine - former * sine_table], axis=-1
    )


def rms_parts(values):
    inv_rms = lax.rsqrt(jnp.mean(values * values, axis=-1, keepdims=True) + EPSILON)
    return (values * inv_rms, inv_rms)


def norm_back(grad_normed, normed, inv_rms, gain):
    grad_gain = jnp.sum(grad_normed * normed, axis=0)
    scaled = grad_normed * gain
    return (
        inv_rms * (scaled - normed * jnp.mean(scaled * normed, axis=-1, keepdims=True)),
        grad_gain,
    )


def local(
    inputs,
    w_query,
    w_key,
    w_value,
    w_out,
    w_gate,
    w_up,
    w_down,
    norm_attn,
    norm_ffn,
    lengths,
    cotangent,
):
    gathered = (
        lax.all_gather(w_query, "fsdp", axis=0, tiled=True),
        lax.all_gather(w_key, "fsdp", axis=0, tiled=True),
        lax.all_gather(w_value, "fsdp", axis=0, tiled=True),
        lax.all_gather(w_out, "fsdp", axis=0, tiled=True),
        lax.all_gather(w_gate, "fsdp", axis=0, tiled=True),
        lax.all_gather(w_up, "fsdp", axis=0, tiled=True),
        lax.all_gather(w_down, "fsdp", axis=0, tiled=True),
        lax.all_gather(norm_attn, "fsdp", axis=0, tiled=True),
        lax.all_gather(norm_ffn, "fsdp", axis=0, tiled=True),
    )
    seq_count, seq_length, model_width = inputs.shape
    head_count = HEADS
    head_width = model_width // head_count
    row_count = seq_count * seq_length
    score_scale = head_width ** (-0.5)
    cosine, sine_table = rotary_tables(seq_length, head_width)
    position = jnp.arange(seq_length, dtype=jnp.int32)
    allowed = (position[None, None, :] <= position[None, :, None]) & (
        position[None, None, :] < lengths[:, None, None]
    )
    shape_heads = (seq_count, seq_length, head_count, head_width)

    def split_heads(values):
        return values.reshape(shape_heads).transpose(2, 0, 1, 3)

    def join_heads(values):
        return values.transpose(1, 2, 0, 3)

    inputs_f = inputs.reshape(row_count, model_width).astype(jnp.float32)
    normed_one, inv_one = rms_parts(inputs_f)
    gain_attn = gathered[7].astype(jnp.float32)
    gain_ffn = gathered[8].astype(jnp.float32)
    h_attn = (normed_one * gain_attn).astype(jnp.bfloat16)
    query_raw = jnp.dot(h_attn, gathered[0], preferred_element_type=jnp.float32)
    key_raw = jnp.dot(h_attn, gathered[1], preferred_element_type=jnp.float32)
    query_heads = split_heads(
        rotate(query_raw.reshape(shape_heads), cosine, sine_table)
        .astype(jnp.bfloat16)
        .reshape(row_count, model_width)
    )
    key_heads = split_heads(
        rotate(key_raw.reshape(shape_heads), cosine, sine_table)
        .astype(jnp.bfloat16)
        .reshape(row_count, model_width)
    )
    value_heads = split_heads(
        jnp.dot(h_attn, gathered[2], preferred_element_type=jnp.float32).astype(jnp.bfloat16)
    )

    def head_forward(operands):
        query_head, key_head, value_head = operands
        scores = (
            jnp.einsum("sqe,ske->sqk", query_head, key_head, preferred_element_type=jnp.float32)
            * score_scale
        )
        scores = jnp.where(allowed, scores, -1e30)
        row_max = jnp.max(scores, axis=-1, keepdims=True)
        exponent = jnp.exp(scores - row_max)
        row_sum = jnp.sum(exponent, axis=-1, keepdims=True)
        attention = (exponent / row_sum).astype(jnp.bfloat16)
        mixed = jnp.einsum(
            "sqk,ske->sqe", attention, value_head, preferred_element_type=jnp.float32
        )
        return (mixed, (row_max + jnp.log(row_sum))[..., 0])

    mixed_heads, log_sums = lax.map(head_forward, (query_heads, key_heads, value_heads))
    mixed_rows = join_heads(mixed_heads.astype(jnp.bfloat16)).reshape(row_count, model_width)
    residual = inputs_f + jnp.dot(mixed_rows, gathered[3], preferred_element_type=jnp.float32)
    normed_two, inv_two = rms_parts(residual)
    h_ffn = (normed_two * gain_ffn).astype(jnp.bfloat16)
    gate_proj = jnp.dot(h_ffn, gathered[4], preferred_element_type=jnp.float32)
    up_proj = jnp.dot(h_ffn, gathered[5], preferred_element_type=jnp.float32)
    sigmoid_gate = jax.nn.sigmoid(gate_proj)
    silu_gate = gate_proj * sigmoid_gate
    hidden = (silu_gate * up_proj).astype(jnp.bfloat16)
    ffn_out = jnp.dot(hidden, gathered[6], preferred_element_type=jnp.float32)
    output = (residual + ffn_out).astype(jnp.bfloat16).reshape(seq_count, seq_length, model_width)
    weights_bk = (
        lax.all_gather(w_query, "fsdp", axis=0, tiled=True),
        lax.all_gather(w_key, "fsdp", axis=0, tiled=True),
        lax.all_gather(w_value, "fsdp", axis=0, tiled=True),
        lax.all_gather(w_out, "fsdp", axis=0, tiled=True),
        lax.all_gather(w_gate, "fsdp", axis=0, tiled=True),
        lax.all_gather(w_up, "fsdp", axis=0, tiled=True),
        lax.all_gather(w_down, "fsdp", axis=0, tiled=True),
        lax.all_gather(norm_attn, "fsdp", axis=0, tiled=True),
        lax.all_gather(norm_ffn, "fsdp", axis=0, tiled=True),
    )
    valid_rows = (position[None, :] < lengths[:, None]).astype(jnp.float32).reshape(row_count, 1)
    grad_output = cotangent.reshape(row_count, model_width).astype(jnp.float32) * valid_rows
    grad_out_b = grad_output.astype(jnp.bfloat16)
    grad_down = jnp.einsum("rf,rd->fd", hidden, grad_out_b, preferred_element_type=jnp.float32)
    grad_hidden = jnp.einsum(
        "rd,fd->rf", grad_out_b, weights_bk[6], preferred_element_type=jnp.float32
    )
    grad_gate_b = (
        grad_hidden * up_proj * sigmoid_gate * (1.0 + gate_proj * (1.0 - sigmoid_gate))
    ).astype(jnp.bfloat16)
    grad_up_b = (grad_hidden * silu_gate).astype(jnp.bfloat16)
    grad_gate = jnp.einsum("rd,rf->df", h_ffn, grad_gate_b, preferred_element_type=jnp.float32)
    grad_up = jnp.einsum("rd,rf->df", h_ffn, grad_up_b, preferred_element_type=jnp.float32)
    grad_h_ffn = jnp.einsum(
        "rf,df->rd", grad_gate_b, weights_bk[4], preferred_element_type=jnp.float32
    )
    grad_h_ffn = grad_h_ffn + jnp.einsum(
        "rf,df->rd", grad_up_b, weights_bk[5], preferred_element_type=jnp.float32
    )
    grad_res_norm, grad_norm_ffn = norm_back(
        grad_h_ffn, normed_two, inv_two, weights_bk[8].astype(jnp.float32)
    )
    grad_residual = grad_output + grad_res_norm
    grad_attn_b = grad_residual.astype(jnp.bfloat16)
    grad_out = jnp.einsum("rd,re->de", mixed_rows, grad_attn_b, preferred_element_type=jnp.float32)
    grad_mixed = jnp.einsum(
        "re,de->rd", grad_attn_b, weights_bk[3], preferred_element_type=jnp.float32
    ).astype(jnp.bfloat16)
    grad_mixed_heads = split_heads(grad_mixed)

    def head_backward(operands):
        query_head, key_head, value_head, grad_head, log_head = operands
        scores = (
            jnp.einsum("sqe,ske->sqk", query_head, key_head, preferred_element_type=jnp.float32)
            * score_scale
        )
        scores = jnp.where(allowed, scores, -1e30)
        attention = jnp.exp(scores - log_head[..., None])
        attention_b = attention.astype(jnp.bfloat16)
        grad_attention = jnp.einsum(
            "sqe,ske->sqk", grad_head, value_head, preferred_element_type=jnp.float32
        )
        grad_scores = (
            attention
            * (grad_attention - jnp.sum(attention * grad_attention, axis=-1, keepdims=True))
        ).astype(jnp.bfloat16)
        grad_query_head = (
            jnp.einsum("sqk,ske->sqe", grad_scores, key_head, preferred_element_type=jnp.float32)
            * score_scale
        )
        grad_key_head = (
            jnp.einsum("sqk,sqe->ske", grad_scores, query_head, preferred_element_type=jnp.float32)
            * score_scale
        )
        grad_value_head = jnp.einsum(
            "sqk,sqe->ske", attention_b, grad_head, preferred_element_type=jnp.float32
        )
        return (grad_query_head, grad_key_head, grad_value_head)

    grad_q_heads, grad_k_heads, grad_v_heads = lax.map(
        head_backward, (query_heads, key_heads, value_heads, grad_mixed_heads, log_sums)
    )
    grad_q_rows = (
        unrotate(join_heads(grad_q_heads), cosine, sine_table)
        .reshape(row_count, model_width)
        .astype(jnp.bfloat16)
    )
    grad_k_rows = (
        unrotate(join_heads(grad_k_heads), cosine, sine_table)
        .reshape(row_count, model_width)
        .astype(jnp.bfloat16)
    )
    grad_v_rows = join_heads(grad_v_heads).reshape(row_count, model_width).astype(jnp.bfloat16)
    grad_query = jnp.einsum("rd,re->de", h_attn, grad_q_rows, preferred_element_type=jnp.float32)
    grad_key = jnp.einsum("rd,re->de", h_attn, grad_k_rows, preferred_element_type=jnp.float32)
    grad_value = jnp.einsum("rd,re->de", h_attn, grad_v_rows, preferred_element_type=jnp.float32)
    grad_h_attn = jnp.einsum(
        "re,de->rd", grad_q_rows, weights_bk[0], preferred_element_type=jnp.float32
    )
    grad_h_attn = grad_h_attn + jnp.einsum(
        "re,de->rd", grad_k_rows, weights_bk[1], preferred_element_type=jnp.float32
    )
    grad_h_attn = grad_h_attn + jnp.einsum(
        "re,de->rd", grad_v_rows, weights_bk[2], preferred_element_type=jnp.float32
    )
    grad_in_norm, grad_norm_attn = norm_back(
        grad_h_attn, normed_one, inv_one, weights_bk[7].astype(jnp.float32)
    )
    grad_input = (
        (grad_residual + grad_in_norm)
        .astype(jnp.bfloat16)
        .reshape(seq_count, seq_length, model_width)
    )
    owned = (
        lax.psum_scatter(grad_query, "fsdp", scatter_dimension=0, tiled=True),
        lax.psum_scatter(grad_key, "fsdp", scatter_dimension=0, tiled=True),
        lax.psum_scatter(grad_value, "fsdp", scatter_dimension=0, tiled=True),
        lax.psum_scatter(grad_out, "fsdp", scatter_dimension=0, tiled=True),
        lax.psum_scatter(grad_gate, "fsdp", scatter_dimension=0, tiled=True),
        lax.psum_scatter(grad_up, "fsdp", scatter_dimension=0, tiled=True),
        lax.psum_scatter(grad_down, "fsdp", scatter_dimension=0, tiled=True),
        lax.psum_scatter(grad_norm_attn, "fsdp", scatter_dimension=0, tiled=True),
        lax.psum_scatter(grad_norm_ffn, "fsdp", scatter_dimension=0, tiled=True),
    )
    reduced = (
        lax.psum(owned[0].astype(jnp.bfloat16), "rep").astype(jnp.float32),
        lax.psum(owned[1].astype(jnp.bfloat16), "rep").astype(jnp.float32),
        lax.psum(owned[2].astype(jnp.bfloat16), "rep").astype(jnp.float32),
        lax.psum(owned[3].astype(jnp.bfloat16), "rep").astype(jnp.float32),
        lax.psum(owned[4].astype(jnp.bfloat16), "rep").astype(jnp.float32),
        lax.psum(owned[5].astype(jnp.bfloat16), "rep").astype(jnp.float32),
        lax.psum(owned[6].astype(jnp.bfloat16), "rep").astype(jnp.float32),
        lax.psum(owned[7].astype(jnp.bfloat16), "rep").astype(jnp.float32),
        lax.psum(owned[8].astype(jnp.bfloat16), "rep").astype(jnp.float32),
    )
    return (
        output,
        grad_input,
        reduced[0],
        reduced[1],
        reduced[2],
        reduced[3],
        reduced[4],
        reduced[5],
        reduced[6],
        reduced[7],
        reduced[8],
    )


def solution(mesh):
    return jax.shard_map(
        local,
        mesh=mesh,
        in_specs=(
            P(("rep", "fsdp"), None, None),
            P("fsdp", None),
            P("fsdp", None),
            P("fsdp", None),
            P("fsdp", None),
            P("fsdp", None),
            P("fsdp", None),
            P("fsdp", None),
            P("fsdp"),
            P("fsdp"),
            P(("rep", "fsdp")),
            P(("rep", "fsdp"), None, None),
        ),
        out_specs=(
            P(("rep", "fsdp"), None, None),
            P(("rep", "fsdp"), None, None),
            P("fsdp", None),
            P("fsdp", None),
            P("fsdp", None),
            P("fsdp", None),
            P("fsdp", None),
            P("fsdp", None),
            P("fsdp", None),
            P("fsdp"),
            P("fsdp"),
        ),
        check_vma=False,
    )
```

profile of v0, /device:TPU:0, one launch (start us, length us, event | category | flops | bytes accessed | tf_op | source)
XLA Modules:
  0.0 832.0 jit_solution(13768503767765881324)
XLA Ops:
  16.6 18.5 %all-reduce.5 = (bf16[768]{0:T(1024)(128)(2,1)S(1)}, bf16[768]{0:T(1024)(128)(2,1)S(1)}) all-reduce(bf16[768]{0:T(1024)(128)(2,1)S(1)} %dynamic-update-slice, bf16[768]{0:T(1024)(128)(2,1)S(1)} %dynamic-update-slice.1), channel_id=1, replica_groups=mesh['rep'=4,'fsdp'=8] {'fsdp'}, use_global_device_ids=true, to_apply=%add | all-reduce | flops 1536 | bytes 6144
  40.6 18.7 %all-gather.8.cloned.1.call-done = bf16[768,768]{1,0:T(8,128)(2,1)} async-done(((bf16[96,768]{1,0:T(8,128)(2,1)}), bf16[768,768]{1,0:T(8,128)(2,1)}) %all-gather.8.cloned.1.call-update) | async-done | bytes 1179664 | tf_op jit(solution)/shard_map/all_gather | solution.py:65
  67.3 4.1 copy.51
  74.2 9.2 %all-gather.12.cloned.1.call-done = bf16[768,768]{1,0:T(8,128)(2,1)} async-done(((bf16[96,768]{1,0:T(8,128)(2,1)}), bf16[768,768]{1,0:T(8,128)(2,1)}) %all-gather.12.cloned.1.call-update) | async-done | bytes 1179664 | tf_op jit(solution)/shard_map/all_gather | solution.py:67
  87.3 4.2 copy.50
  91.6 68.2 %while.30 = (s32[]{:T(128)}, bf16[12,1,1024,64]{2,3,1,0:T(8,128)(2,1)S(1)}, f32[12,1,1024]{2,1,0:T(1,128)S(1)}, bf16[12,1,1024,64]{3,2,1,0:T(8,128)(2,1)}, bf16[...) while((s32[]{:T(128)}, ...), condition=%wide.region_4.5_spmd.clone.clone, body=%wide.region_1.4_spmd.clone.sunk.clone | while | flops 287308800 | bytes 13677649 | solution.py:130
  165.9 9.2 %fusion.106 = f32[1024,2048]{1,0:T(8,128)} fusion(bf16[1024,768]{0,1:T(8,128)(2,1)} %multiply_convert_fusion.4, bf16[768,2048]{1,0:T(8,128)(2,1)} %all-gather.16.cloned.1.call-done), kind=kOutput, calls=%fused_computation.144 | convolution fusion | flops 3221225472 | bytes 13107200 | tf_op jit(solution)/shard_map/dot_general | solution.py:135
  175.0 10.3 %all-gather.18.cloned.1.call-done = bf16[768,2048]{1,0:T(8,128)(2,1)} async-done(((bf16[96,2048]{1,0:T(8,128)(2,1)}), bf16[768,2048]{1,0:T(8,128)(2,1)}) %all-gather.18.cloned.1.call-update) | async-done | bytes 3145744 | tf_op jit(solution)/shard_map/all_gather | solution.py:70
  185.4 9.2 %fusion.107 = f32[1024,2048]{1,0:T(8,128)} fusion(bf16[1024,768]{0,1:T(8,128)(2,1)} %multiply_convert_fusion.4, bf16[768,2048]{1,0:T(8,128)(2,1)} %all-gather.18.cloned.1.call-done), kind=kOutput, calls=%fused_computation.145 | convolution fusion | flops 3221225472 | bytes 13107200 | tf_op jit(solution)/shard_map/dot_general | solution.py:136
  194.6 29.6 %all-gather.20.cloned.1.call-done = bf16[2048,768]{1,0:T(8,128)(2,1)} async-done(((bf16[256,768]{1,0:T(8,128)(2,1)}), bf16[2048,768]{1,0:T(8,128)(2,1)}) %all-gather.20.cloned.1.call-update) | async-done | bytes 3145744 | tf_op jit(solution)/shard_map/all_gather | solution.py:71
  224.2 14.8 %multiply_convert_fusion.1 = (bf16[1024,2048]{1,0:T(8,128)(2,1)S(1)}, bf16[1024,2048]{1,0:T(8,128)(2,1)}, bf16[1024,2048]{1,0:T(8,128)(2,1)}) fusion(f32[1024,2048]{1,0:T(8,128)} %fusion.106, f32[1024,2048]{1,0:T(8,128)} %fusion.107, bf16[2048,768]{1,0:T(8,128)(2,1)} %all-gather.20.cloned.1.call-done, bf16[1,1024,768]{1,2,0:T(8,128)(2,1)} %copy.54, ...), kind=kOutput, calls=%fused_computation.63 | convolution fusion | flops 3255042048 | bytes 34082816 | tf_op jit(solution)/shard_map/rd,fd->rf/dot_general | solution.py:157
  239.0 7.4 fusion.108
  246.4 4.0 multiply_reduce_fusion.1
  255.8 4.8 convolution_convert_fusion
  260.7 4.3 copy.57
  265.0 149.9 %while.31 = (s32[]{:T(128)}, f32[12,1,1024,64]{2,3,1,0:T(8,128)}, f32[12,1,1024,64]{2,3,1,0:T(8,128)}, bf16[12,1,1024,64]{2,3,1,0:T(8,128)(2,1)S(1)}, bf16[12,1,...) while((s32[]{:T(128)}, f32[12,1,1024,64]{2,3,1,0:T(8,128)}, ...), condition=%wide.region_9.10_spmd.clone.clone, body=%wide.region_7.9_spmd.clone.sunk.clone | while | flops 682753024 | bytes 34105448 | solution.py:212
  414.9 5.0 multiply_add_fusion
  432.8 8.7 %fusion.109 = f32[768,2048]{1,0:T(8,128)} fusion(bf16[1024,768]{0,1:T(8,128)(2,1)} %multiply_convert_fusion.4, bf16[1024,2048]{1,0:T(8,128)(2,1)} %get-tuple-element.260), kind=kOutput, calls=%fused_computation.147 | convolution fusion | flops 3221225472 | bytes 12058624 | tf_op jit(solution)/shard_map/rd,rf->df/dot_general | solution.py:164
  441.8 8.7 %fusion.110 = f32[768,2048]{1,0:T(8,128)} fusion(bf16[1024,768]{0,1:T(8,128)(2,1)} %multiply_convert_fusion.4, bf16[1024,2048]{1,0:T(8,128)(2,1)} %copy-done.30), kind=kOutput, calls=%fused_computation.148 | convolution fusion | flops 3221225472 | bytes 12058624 | tf_op jit(solution)/shard_map/rd,rf->df/dot_general | solution.py:165
  450.6 8.9 %fusion.89 = f32[2048,768]{1,0:T(8,128)} fusion(bf16[1024,2048]{1,0:T(8,128)(2,1)} %get-tuple-element.261, bf16[1,1024,768]{1,2,0:T(8,128)(2,1)} %copy.54, f32[1024]{0:T(1024)S(1)} %fusion.98), kind=kOutput, calls=%fused_computation.125 | convolution fusion | flops 3223584768 | bytes 12062720 | tf_op jit(solution)/shard_map/rf,rd->fd/dot_general | solution.py:156
  460.3 5.0 fusion.112
  471.6 26.8 %reduce-scatter.8.cloned.1.call-done = f32[96,768]{1,0:T(8,128)} async-done(((f32[768,768]{1,0:T(8,128)}), f32[96,768]{1,0:T(8,128)}) %reduce-scatter.8.cloned.1.call-update) | async-done | bytes 294928 | tf_op jit(solution)/shard_map/reduce_scatter | solution.py:247
  500.0 36.7 %reduce-scatter.12.cloned.1.call-done = f32[96,768]{1,0:T(8,128)} async-done(((f32[768,768]{1,0:T(8,128)}), f32[96,768]{1,0:T(8,128)}) %reduce-scatter.12.cloned.1.call-update) | async-done | bytes 294928 | tf_op jit(solution)/shard_map/reduce_scatter | solution.py:249
  538.4 69.1 %reduce-scatter.16.cloned.1.call-done = f32[96,2048]{1,0:T(8,128)} async-done(((f32[768,2048]{1,0:T(8,128)}), f32[96,2048]{1,0:T(8,128)}) %reduce-scatter.16.cloned.1.call-update) | async-done | bytes 786448 | tf_op jit(solution)/shard_map/reduce_scatter | solution.py:251
  609.4 68.6 %reduce-scatter.18.cloned.1.call-done = f32[96,2048]{1,0:T(8,128)} async-done(((f32[768,2048]{1,0:T(8,128)}), f32[96,2048]{1,0:T(8,128)}) %reduce-scatter.18.cloned.1.call-update) | async-done | bytes 786448 | tf_op jit(solution)/shard_map/reduce_scatter | solution.py:252
  679.9 68.4 %reduce-scatter.20.cloned.1.call-done = f32[256,768]{1,0:T(8,128)} async-done(((f32[2048,768]{1,0:T(8,128)}), f32[256,768]{1,0:T(8,128)}) %reduce-scatter.20.cloned.1.call-update) | async-done | bytes 786448 | tf_op jit(solution)/shard_map/reduce_scatter | solution.py:253
  750.3 6.6 fusion.70
  756.9 13.9 %all-reduce.4 = (bf16[768]{0:T(1024)(128)(2,1)S(1)}, bf16[768]{0:T(1024)(128)(2,1)S(1)}) all-reduce(f32[768]{0:T(1024)S(1)} %get-tuple-element.206, f32[768]{0:T(1024)S(1)} %get-tuple-element.204), channel_id=9, replica_groups=mesh['rep'=4,'fsdp'=8] {'fsdp'}, use_global_device_ids=true, to_apply=%region_26.27.clone | all-reduce | flops 1536 | bytes 9216
  771.0 10.5 %all-reduce.6 = (bf16[96]{0:T(256)(128)(2,1)S(1)}, bf16[96]{0:T(256)(128)(2,1)S(1)}) all-reduce(bf16[96]{0:T(256)(128)(2,1)S(1)} %dynamic-slice.9, bf16[96]{0:T(256)(128)(2,1)S(1)} %dynamic-slice.8), channel_id=1, replica_groups=mesh['rep'=4,'fsdp'=8] {'rep'}, use_global_device_ids=true, to_apply=%region_27.28 | all-reduce | flops 192 | bytes 768 | tf_op jit(solution)/shard_map/psum | solution.py:265
  782.5 4.8 fusion.76
  790.1 8.0 fusion.88
  800.7 15.6 %all-reduce.10.cloned.1.call-done = (bf16[96,768]{1,0:T(8,128)(2,1)}, bf16[96,768]{1,0:T(8,128)(2,1)}, bf16[96,768]{1,0:T(8,128)(2,1)}, bf16[96,768]{1,0:T(8,128...) async-done(((bf16[96,768]{1,0:T(8,128)(2,1)}, bf16[96,768]{1,0:T(8,128)(2,1)}, bf16[96,768]{1,0:T(8,128)(2,1)}, ...) | async-done | bytes 1769488 | tf_op jit(solution)/shard_map/psum | solution.py:258
  (301 shorter events, 300.1 us)
Async XLA Ops:
  7.2 31.8 %all-gather.10.cloned.1.call-start = ((), (), s32[]{:S(2)}) async-start(), calls=%async_computation.8 | async-start | bytes 1327104 | tf_op jit(solution)/shard_map/all_gather | solution.py:66
  7.9 51.4 %all-gather.8.cloned.1.call-start = ((), (), s32[]{:S(2)}) async-start(), calls=%async_computation.7 | async-start | bytes 1327104 | tf_op jit(solution)/shard_map/all_gather | solution.py:65
  8.7 74.7 %all-gather.12.cloned.1.call-start = ((), (), s32[]{:S(2)}) async-start(), calls=%async_computation.9 | async-start | bytes 1327104 | tf_op jit(solution)/shard_map/all_gather | solution.py:67
  9.4 150.4 %all-gather.14.cloned.1.call-start = ((), (), s32[]{:S(2)}) async-start(), calls=%async_computation.10 | async-start | bytes 1327104 | tf_op jit(solution)/shard_map/all_gather | solution.py:68
  10.0 155.9 %all-gather.16.cloned.1.call-start = ((), (), s32[]{:S(2)}) async-start(), calls=%async_computation.11 | async-start | bytes 3538944 | tf_op jit(solution)/shard_map/all_gather | solution.py:69
  10.6 174.8 %all-gather.18.cloned.1.call-start = ((), (), s32[]{:S(2)}) async-start(), calls=%async_computation.12 | async-start | bytes 3538944 | tf_op jit(solution)/shard_map/all_gather | solution.py:70
  11.1 213.0 %all-gather.20.cloned.1.call-start = ((), (), s32[]{:S(2)}) async-start(), calls=%async_computation.13 | async-start | bytes 3538944 | tf_op jit(solution)/shard_map/all_gather | solution.py:71
  11.9 456.4 %reduce-scatter.14.cloned.1.call-start = ((), (), s32[]{:S(2)}) async-start(), calls=%async_computation.17 | async-start | bytes 2654208 | tf_op jit(solution)/shard_map/reduce_scatter | solution.py:250
  12.2 24.2 %copy-start = (bf16[12,1,1024,64]{2,3,1,0:T(8,128)(2,1)}, bf16[12,1,1024,64]{2,3,1,0:T(8,128)(2,1)S(1)}, u32[]{:S(2)}) copy-start(bf16[12,1,1024,64]{2,3,1,0:T(8,128)(2,1)S(1)} %fusion.104) | copy-start | bytes 4718596
  14.9 68.5 %copy-start.21 = (f32[1024]{0:T(1024)}, f32[1024]{0:T(1024)S(1)}, u32[]{:S(2)}) copy-start(f32[1024]{0:T(1024)S(1)} %add_rsqrt_fusion.1) | copy-start | bytes 12292
  35.1 48.3 %copy-start.23 = (f32[768]{0:T(1024)}, f32[768]{0:T(1024)S(1)}, u32[]{:S(2)}) copy-start(f32[768]{0:T(1024)S(1)} %convert_element_type.215) | copy-start | bytes 9220
  35.6 29.1 %copy-start.11 = (f32[1024,32]{0,1:T(8,128)}, f32[1024,32]{0,1:T(8,128)S(1)}, u32[]{:S(2)}) copy-start(f32[1024,32]{0,1:T(8,128)S(1)} %get-tuple-element.278) | copy-start | bytes 393220
  35.7 29.1 %copy-start.13 = (f32[1024,32]{0,1:T(8,128)}, f32[1024,32]{0,1:T(8,128)S(1)}, u32[]{:S(2)}) copy-start(f32[1024,32]{0,1:T(8,128)S(1)} %get-tuple-element.279) | copy-start | bytes 393220
  224.2 14.8 %copy-start.26 = (bf16[768,2048]{1,0:T(8,128)(2,1)S(1)}, bf16[768,2048]{1,0:T(8,128)(2,1)}, u32[]{:S(2)}) copy-start(bf16[768,2048]{1,0:T(8,128)(2,1)} %all-gather.16.cloned.1.call-done) | copy-start | bytes 9437188
  239.0 7.4 copy-start.30
  239.0 7.4 copy-start.5
  239.0 7.4 copy-start.27
  264.9 205.0 %reduce-scatter.10.cloned.1.call-start = ((), (), s32[]{:S(2)}) async-start(), calls=%async_computation.15 | async-start | bytes 2654208 | tf_op jit(solution)/shard_map/reduce_scatter | solution.py:248
  265.0 149.9 %copy-start.12 = (f32[1024,32]{0,1:T(8,128)S(1)}, f32[1024,32]{0,1:T(8,128)}, u32[]{:S(2)}) copy-start(f32[1024,32]{0,1:T(8,128)} %copy-done.11) | copy-start | bytes 393220
  265.0 149.9 %copy-start.14 = (f32[1024,32]{0,1:T(8,128)S(1)}, f32[1024,32]{0,1:T(8,128)}, u32[]{:S(2)}) copy-start(f32[1024,32]{0,1:T(8,128)} %copy-done.13) | copy-start | bytes 393220
  424.1 74.3 %reduce-scatter.8.cloned.1.call-start = ((), (), s32[]{:S(2)}) async-start(), calls=%async_computation.14 | async-start | bytes 2654208 | tf_op jit(solution)/shard_map/reduce_scatter | solution.py:247
  429.7 107.0 %reduce-scatter.12.cloned.1.call-start = ((), (), s32[]{:S(2)}) async-start(), calls=%async_computation.16 | async-start | bytes 2654208 | tf_op jit(solution)/shard_map/reduce_scatter | solution.py:249
  432.7 174.8 %reduce-scatter.16.cloned.1.call-start = ((), (), s32[]{:S(2)}) async-start(), calls=%async_computation.18 | async-start | bytes 7077888 | tf_op jit(solution)/shard_map/reduce_scatter | solution.py:251
  441.5 236.5 %reduce-scatter.18.cloned.1.call-start = ((), (), s32[]{:S(2)}) async-start(), calls=%async_computation.19 | async-start | bytes 7077888 | tf_op jit(solution)/shard_map/reduce_scatter | solution.py:252
  450.6 297.8 %reduce-scatter.20.cloned.1.call-start = ((), (), s32[]{:S(2)}) async-start(), calls=%async_computation.20 | async-start | bytes 7077888 | tf_op jit(solution)/shard_map/reduce_scatter | solution.py:253
  459.5 356.7 %all-reduce.10.cloned.1.call-start = ((), (), s32[]{:S(2)}) async-start(), calls=%async_computation.21 | async-start | bytes 3538944 | tf_op jit(solution)/shard_map/psum | solution.py:258
  460.2 5.1 copy-start.10
  460.3 5.0 copy-start.15
  816.2 5.9 copy-start.20
  816.2 6.6 copy-start.19
  816.2 7.4 copy-start.18
  816.2 8.1 copy-start.17
  (14 other events, 36.6 us)
Sparse Core Ops, SparseCore 0:
  9.6 25.6 all-gather.9
  37.0 22.2 all-gather.7
  60.9 22.4 all-gather.11
  84.9 22.4 all-gather.13
  108.8 37.8 all-gather.15
  148.2 37.1 all-gather.17
  187.0 37.1 all-gather.19
  265.1 35.9 reduce-scatter.13
  424.2 35.9 reduce-scatter.9
  462.4 35.9 reduce-scatter.7
  500.7 35.9 reduce-scatter.11
  538.9 68.5 reduce-scatter.15
  609.8 68.1 reduce-scatter.17
  680.2 68.1 reduce-scatter.19
  753.3 62.8 all-reduce.9
where the time goes:
time: 844 us; the launch traced here: 832 us
  waiting for transfers between devices  358 us (42%)
  matrix products  299 us (35%)
  other arithmetic  76.5 us (9%)
  blocking collectives  42.9 us (5%)
  local copies, waits for them, and re-layouts  36.6 us (4%)
  between operations  16.9 us (2%)
    reduce_scatter x1, waiting for transfers between devices, local(): lax.psum_scatter(grad_gate, 'fsdp', scatter_dimension=0, tiled=True)  69.1 us
    reduce_scatter x1, waiting for transfers between devices, local(): lax.psum_scatter(grad_up, 'fsdp', scatter_dimension=0, tiled=True)  68.6 us
    reduce_scatter x1, waiting for transfers between devices, local(): lax.psum_scatter(grad_down, 'fsdp', scatter_dimension=0, tiled=True)  68.4 us
    dot_general x12, matrix products, head_backward(): jnp.einsum('sqe,ske->sqk', query_head, key_head, preferred_element_type=j...  38.4 us
    reduce_scatter x1, waiting for transfers between devices, local(): lax.psum_scatter(grad_value, 'fsdp', scatter_dimension=0, tiled=True)  36.7 us
    unnamed x2, blocking collectives  32.4 us
    all_gather x1, waiting for transfers between devices, local(): lax.all_gather(w_down, 'fsdp', axis=0, tiled=True)  29.6 us
    dot_general x12, matrix products, head_backward(): jnp.einsum('sqk,sqe->ske', grad_scores, query_head, preferred_element_typ...  29.3 us
  transfers between devices with their start and end apart: 15, of which 10 were waited for; matrix products, arithmetic and copies ran while one was open for 43% of the time, Pallas kernels for 0%

commit v1 on v0

--- a/solution.py
+++ b/solution.py
@@ -5,6 +5,18 @@
 
 HEADS = 12
 EPSILON = 1e-05
+
+
+def gather_by_bits(x, axis, dim):
+    ways, here = (lax.axis_size(axis), lax.axis_index(axis))
+    grown, reach = (x, 1)
+    while reach < ways:
+        theirs = lax.ppermute(grown, axis, [(d, d ^ reach) for d in range(ways)])
+        mine_first = jnp.concatenate([grown, theirs], axis=dim)
+        theirs_first = jnp.concatenate([theirs, grown], axis=dim)
+        grown = jnp.where(here & reach == 0, mine_first, theirs_first)
+        reach = 2 * reach
+    return grown
 
 
 def rotary_tables(seq_length, head_width):
@@ -62,7 +74,7 @@
     cotangent,
 ):
     gathered = (
-        lax.all_gather(w_query, "fsdp", axis=0, tiled=True),
+        gather_by_bits(w_query, "fsdp", 0),
         lax.all_gather(w_key, "fsdp", axis=0, tiled=True),
         lax.all_gather(w_value, "fsdp", axis=0, tiled=True),
         lax.all_gather(w_out, "fsdp", axis=0, tiled=True),

time: 844 us -> 819 us (0.970)
  waiting for transfers between devices: 358 us -> 329 us
    ppermute x0 -> x3, waiting for transfers between devices: none -> 20.8 us  [gather_by_bits(): theirs = lax.ppermute(grown, axis, [(d, d ^ reach) for d in range(ways)])]
    all_gather x1, waiting for transfers between devices: 18.7 us -> 0.01 us  [local(): lax.all_gather(w_query, 'fsdp', axis=0, tiled=True)]
    all_gather x1, waiting for transfers between devices: 29.6 us -> 17.8 us  [local(): lax.all_gather(w_down, 'fsdp', axis=0, tiled=True)]
    all_gather x1, waiting for transfers between devices: 10.3 us -> 0.01 us  [local(): lax.all_gather(w_up, 'fsdp', axis=0, tiled=True)]
    all_gather x1, waiting for transfers between devices: 9.23 us -> 0.01 us  [local(): lax.all_gather(w_value, 'fsdp', axis=0, tiled=True)]
    unnamed x75 -> x78, local copies, waits for them, and re-layouts: 23.9 us -> 21.7 us
  transfers between devices with their start and end apart: 15 -> 18, of which waited for: 10 -> 9; matrix products, arithmetic and copies ran while one was open for 43% -> 48% of each run, Pallas kernels for 0% -> 0%
where the time goes in v1:
time: 819 us; the launch traced here: 813 us
  waiting for transfers between devices  329 us (40%)
  matrix products  299 us (37%)
  other arithmetic  78 us (10%)
  blocking collectives  49.6 us (6%)
  local copies, waits for them, and re-layouts  30.5 us (4%)
  between operations  16.7 us (2%)
  starting transfers between devices  8.65 us (1%)
    reduce_scatter x1, waiting for transfers between devices, local(): lax.psum_scatter(grad_gate, 'fsdp', scatter_dimension=0, tiled=True)  69.2 us
    reduce_scatter x1, waiting for transfers between devices, local(): lax.psum_scatter(grad_up, 'fsdp', scatter_dimension=0, tiled=True)  68.6 us
    reduce_scatter x1, waiting for transfers between devices, local(): lax.psum_scatter(grad_down, 'fsdp', scatter_dimension=0, tiled=True)  68.5 us
    unnamed x2, blocking collectives  39 us
    dot_general x12, matrix products, head_backward(): jnp.einsum('sqe,ske->sqk', query_head, key_head, preferred_element_type=j...  38.4 us
    reduce_scatter x1, waiting for transfers between devices, local(): lax.psum_scatter(grad_value, 'fsdp', scatter_dimension=0, tiled=True)  36.6 us
    dot_general x12, matrix products, head_backward(): jnp.einsum('sqk,sqe->ske', grad_scores, query_head, preferred_element_typ...  29.2 us
    dot_general x12, matrix products, head_backward(): jnp.einsum('sqk,ske->sqe', grad_scores, key_head, preferred_element_type=...  26.3 us
  transfers between devices with their start and end apart: 18, of which 9 were waited for; matrix products, arithmetic and copies ran while one was open for 48% of the time, Pallas kernels for 0%

profile of v1, /device:TPU:0, one launch (start us, length us, event | category | flops | bytes accessed | tf_op | source)
XLA Modules:
  0.0 813.0 jit_solution(10860290471594164008)
XLA Ops:
  18.0 15.9 %collective-permute-done.1 = bf16[192,768]{0,1:T(8,128)(2,1)S(1)} collective-permute-done((bf16[192,768]{0,1:T(8,128)(2,1)S(1)}, bf16[192,768]{0,1:T(8,128)(2,1)S(1)}, u32[]{:S(2)}, u32[]{:S(2)}) %collective-permute-start.1) | collective-permute-done | bytes 294944 | tf_op jit(solution)/shard_map/ppermute | solution.py:14
  35.2 4.6 collective-permute-start.2
  41.6 25.1 %all-reduce.5 = (bf16[768]{0:T(1024)(128)(2,1)S(1)}, bf16[768]{0:T(1024)(128)(2,1)S(1)}) all-reduce(bf16[768]{0:T(1024)(128)(2,1)S(1)} %dynamic-update-slice, bf16[768]{0:T(1024)(128)(2,1)S(1)} %dynamic-update-slice.1), channel_id=1, replica_groups=mesh['rep'=4,'fsdp'=8] {'fsdp'}, use_global_device_ids=true, to_apply=%add | all-reduce | flops 1536 | bytes 6144
  70.0 4.9 collective-permute-done.2
  86.1 4.1 copy.77
  92.9 3.9 convolution_convert_fusion.1
  96.8 4.2 copy.76
  101.1 68.3 %while.30 = (s32[]{:T(128)}, bf16[12,1,1024,64]{2,3,1,0:T(8,128)(2,1)S(1)}, f32[12,1,1024]{2,1,0:T(1,128)S(1)}, bf16[12,1,1024,64]{3,2,1,0:T(8,128)(2,1)}, bf16[...) while((s32[]{:T(128)}, ...), condition=%wide.region_4.5_spmd.clone.clone, body=%wide.region_1.4_spmd.clone.sunk.clone | while | flops 287308800 | bytes 13677649 | solution.py:142
  176.0 7.6 fusion.106
  183.6 9.2 %fusion.107 = f32[1024,2048]{1,0:T(8,128)} fusion(bf16[1024,768]{0,1:T(8,128)(2,1)} %copy-done.12, bf16[768,2048]{1,0:T(8,128)(2,1)} %all-gather.16.cloned.1.call-done), kind=kOutput, calls=%fused_computation.148 | convolution fusion | flops 3221225472 | bytes 13107200 | tf_op jit(solution)/shard_map/dot_general | solution.py:148
  192.8 17.8 %all-gather.18.cloned.1.call-done = bf16[2048,768]{1,0:T(8,128)(2,1)} async-done(((bf16[256,768]{1,0:T(8,128)(2,1)}), bf16[2048,768]{1,0:T(8,128)(2,1)}) %all-gather.18.cloned.1.call-update) | async-done | bytes 3145744 | tf_op jit(solution)/shard_map/all_gather | solution.py:83
  210.6 13.2 %multiply_convert_fusion.1 = (bf16[1024,2048]{1,0:T(8,128)(2,1)S(1)}, bf16[1024,2048]{1,0:T(8,128)(2,1)}, bf16[1024,2048]{1,0:T(8,128)(2,1)}) fusion(f32[1024,2048]{1,0:T(8,128)} %fusion.106, f32[1024,2048]{1,0:T(8,128)} %fusion.107, bf16[2048,768]{1,0:T(8,128)(2,1)} %all-gather.18.cloned.1.call-done, bf16[1,1024,768]{1,2,0:T(8,128)(2,1)S(1)} %copy-done.7, ...), kind=kOutput, calls=%fused_computation.63 | convolution fusion | flops 3255042048 | bytes 34082816 | tf_op jit(solution)/shard_map/rd,fd->rf/dot_general | solution.py:169
  223.9 7.2 fusion.108
  231.1 4.0 multiply_reduce_fusion.1
  240.8 5.4 fusion.93
  246.2 149.8 %while.31 = (s32[]{:T(128)}, f32[12,1,1024,64]{2,3,1,0:T(8,128)}, f32[12,1,1024,64]{2,3,1,0:T(8,128)}, bf16[12,1,1024,64]{2,3,1,0:T(8,128)(2,1)S(1)}, bf16[12,1,...) while((s32[]{:T(128)}, f32[12,1,1024,64]{2,3,1,0:T(8,128)}, ...), condition=%wide.region_9.10_spmd.clone.clone, body=%wide.region_7.9_spmd.clone.sunk.clone | while | flops 682753024 | bytes 34105448 | solution.py:224
  396.1 5.0 multiply_add_fusion
  413.9 8.7 %fusion.109 = f32[768,2048]{1,0:T(8,128)} fusion(bf16[1024,768]{0,1:T(8,128)(2,1)} %copy-done.12, bf16[1024,2048]{1,0:T(8,128)(2,1)} %get-tuple-element.288), kind=kOutput, calls=%fused_computation.150 | convolution fusion | flops 3221225472 | bytes 12058624 | tf_op jit(solution)/shard_map/rd,rf->df/dot_general | solution.py:176
  423.0 8.7 %fusion.110 = f32[768,2048]{1,0:T(8,128)} fusion(bf16[1024,768]{0,1:T(8,128)(2,1)} %copy-done.12, bf16[1024,2048]{1,0:T(8,128)(2,1)} %copy-done.31), kind=kOutput, calls=%fused_computation.151 | convolution fusion | flops 3221225472 | bytes 12058624 | tf_op jit(solution)/shard_map/rd,rf->df/dot_general | solution.py:177
  431.8 8.9 %fusion.89 = f32[2048,768]{1,0:T(8,128)} fusion(bf16[1024,2048]{1,0:T(8,128)(2,1)} %get-tuple-element.289, bf16[1,1024,768]{1,2,0:T(8,128)(2,1)} %copy.80, f32[1024]{0:T(1024)S(1)} %fusion.98), kind=kOutput, calls=%fused_computation.125 | convolution fusion | flops 3223584768 | bytes 12062720 | tf_op jit(solution)/shard_map/rf,rd->fd/dot_general | solution.py:168
  441.4 4.9 fusion.112
  446.3 4.8 fusion.111
  454.3 25.2 %reduce-scatter.8.cloned.1.call-done = f32[96,768]{1,0:T(8,128)} async-done(((f32[768,768]{1,0:T(8,128)}), f32[96,768]{1,0:T(8,128)}) %reduce-scatter.8.cloned.1.call-update) | async-done | bytes 294928 | tf_op jit(solution)/shard_map/reduce_scatter | solution.py:259
  481.1 36.6 %reduce-scatter.12.cloned.1.call-done = f32[96,768]{1,0:T(8,128)} async-done(((f32[768,768]{1,0:T(8,128)}), f32[96,768]{1,0:T(8,128)}) %reduce-scatter.12.cloned.1.call-update) | async-done | bytes 294928 | tf_op jit(solution)/shard_map/reduce_scatter | solution.py:261
  519.4 69.2 %reduce-scatter.16.cloned.1.call-done = f32[96,2048]{1,0:T(8,128)} async-done(((f32[768,2048]{1,0:T(8,128)}), f32[96,2048]{1,0:T(8,128)}) %reduce-scatter.16.cloned.1.call-update) | async-done | bytes 786448 | tf_op jit(solution)/shard_map/reduce_scatter | solution.py:263
  590.6 68.6 %reduce-scatter.18.cloned.1.call-done = f32[96,2048]{1,0:T(8,128)} async-done(((f32[768,2048]{1,0:T(8,128)}), f32[96,2048]{1,0:T(8,128)}) %reduce-scatter.18.cloned.1.call-update) | async-done | bytes 786448 | tf_op jit(solution)/shard_map/reduce_scatter | solution.py:264
  661.1 68.5 %reduce-scatter.20.cloned.1.call-done = f32[256,768]{1,0:T(8,128)} async-done(((f32[2048,768]{1,0:T(8,128)}), f32[256,768]{1,0:T(8,128)}) %reduce-scatter.20.cloned.1.call-update) | async-done | bytes 786448 | tf_op jit(solution)/shard_map/reduce_scatter | solution.py:265
  731.5 6.6 fusion.70
  738.0 13.9 %all-reduce.4 = (bf16[768]{0:T(1024)(128)(2,1)S(1)}, bf16[768]{0:T(1024)(128)(2,1)S(1)}) all-reduce(f32[768]{0:T(1024)S(1)} %get-tuple-element.234, f32[768]{0:T(1024)S(1)} %get-tuple-element.232), channel_id=9, replica_groups=mesh['rep'=4,'fsdp'=8] {'fsdp'}, use_global_device_ids=true, to_apply=%region_26.27.clone | all-reduce | flops 1536 | bytes 9216
  752.1 10.5 %all-reduce.6 = (bf16[96]{0:T(256)(128)(2,1)S(1)}, bf16[96]{0:T(256)(128)(2,1)S(1)}) all-reduce(bf16[96]{0:T(256)(128)(2,1)S(1)} %dynamic-slice.9, bf16[96]{0:T(256)(128)(2,1)S(1)} %dynamic-slice.8), channel_id=1, replica_groups=mesh['rep'=4,'fsdp'=8] {'rep'}, use_global_device_ids=true, to_apply=%region_27.28 | all-reduce | flops 192 | bytes 768 | tf_op jit(solution)/shard_map/psum | solution.py:277
  768.9 7.9 fusion.88
  778.4 19.0 %all-reduce.10.cloned.1.call-done = (bf16[96,768]{1,0:T(8,128)(2,1)}, bf16[96,768]{1,0:T(8,128)(2,1)}, bf16[96,768]{1,0:T(8,128)(2,1)}, bf16[96,768]{1,0:T(8,128...) async-done(((bf16[96,768]{1,0:T(8,128)(2,1)}, bf16[96,768]{1,0:T(8,128)(2,1)}, bf16[96,768]{1,0:T(8,128)(2,1)}, ...) | async-done | bytes 1769488 | tf_op jit(solution)/shard_map/psum | solution.py:270
  (312 shorter events, 300.8 us)
Async XLA Ops:
  7.2 72.8 %all-gather.8.cloned.1.call-start = ((), (), s32[]{:S(2)}) async-start(), calls=%async_computation.7 | async-start | bytes 1327104 | tf_op jit(solution)/shard_map/all_gather | solution.py:78
  7.9 85.0 %all-gather.10.cloned.1.call-start = ((), (), s32[]{:S(2)}) async-start(), calls=%async_computation.8 | async-start | bytes 1327104 | tf_op jit(solution)/shard_map/all_gather | solution.py:79
  8.7 160.7 %all-gather.12.cloned.1.call-start = ((), (), s32[]{:S(2)}) async-start(), calls=%async_computation.9 | async-start | bytes 1327104 | tf_op jit(solution)/shard_map/all_gather | solution.py:80
  9.4 165.4 %all-gather.14.cloned.1.call-start = ((), (), s32[]{:S(2)}) async-start(), calls=%async_computation.10 | async-start | bytes 3538944 | tf_op jit(solution)/shard_map/all_gather | solution.py:81
  10.0 173.6 %all-gather.16.cloned.1.call-start = ((), (), s32[]{:S(2)}) async-start(), calls=%async_computation.11 | async-start | bytes 3538944 | tf_op jit(solution)/shard_map/all_gather | solution.py:82
  10.6 200.0 %all-gather.18.cloned.1.call-start = ((), (), s32[]{:S(2)}) async-start(), calls=%async_computation.12 | async-start | bytes 3538944 | tf_op jit(solution)/shard_map/all_gather | solution.py:83
  11.1 435.1 %all-gather.20.cloned.1.call-start = ((), (), s32[]{:S(2)}) async-start(), calls=%async_computation.13 | async-start | bytes 1327104 | tf_op jit(solution)/shard_map/all_gather | solution.py:155
  12.3 2.3 collective-permute-start
  12.9 438.2 %reduce-scatter.14.cloned.1.call-start = ((), (), s32[]{:S(2)}) async-start(), calls=%async_computation.17 | async-start | bytes 2654208 | tf_op jit(solution)/shard_map/reduce_scatter | solution.py:262
  13.7 26.2 %copy-start.25 = (u32[32]{0:T(128)S(1)}, u32[32]{0:T(128)}, u32[]{:S(2)}) copy-start(u32[32]{0:T(128)} %constant.80) | copy-start | bytes 388
  13.7 27.4 %copy-start.29 = (bf16[96]{0:T(256)(128)(2,1)S(1)}, bf16[96]{0:T(256)(128)(2,1)}, u32[]{:S(2)}) copy-start(bf16[96]{0:T(256)(128)(2,1)} %param.24) | copy-start | bytes 580
  13.7 27.7 %copy-start.30 = (bf16[96]{0:T(256)(128)(2,1)S(1)}, bf16[96]{0:T(256)(128)(2,1)}, u32[]{:S(2)}) copy-start(bf16[96]{0:T(256)(128)(2,1)} %param.25) | copy-start | bytes 580
  14.6 52.2 %copy-start = (bf16[12,1,1024,64]{2,3,1,0:T(8,128)(2,1)}, bf16[12,1,1024,64]{2,3,1,0:T(8,128)(2,1)S(1)}, u32[]{:S(2)}) copy-start(bf16[12,1,1024,64]{2,3,1,0:T(8,128)(2,1)S(1)} %fusion.104) | copy-start | bytes 4718596
  15.0 18.9 %collective-permute-start.1 = (bf16[192,768]{0,1:T(8,128)(2,1)S(1)}, bf16[192,768]{0,1:T(8,128)(2,1)S(1)}, u32[]{:S(2)}, u32[]{:S(2)}) collective-permute-start(bf16[192,768]{0,1:T(8,128)(2,1)S(1)} %maximum_select_fusion.2), channel_id=1, source_target_pairs={{0,2},{1,3},{2,0},{3,1},{4,6},{5,7},{6,4},{7,5},{8,10},{9,11},{10,... | collective-permute-start | bytes 884744 | tf_op jit(solution)/shard_map/ppermute | solution.py:14
  35.2 39.7 %collective-permute-start.2 = (bf16[384,768]{0,1:T(8,128)(2,1)}, bf16[384,768]{0,1:T(8,128)(2,1)}, u32[]{:S(2)}, u32[]{:S(2)}) collective-permute-start(bf16[384,768]{0,1:T(8,128)(2,1)} %maximum_select_fusion.1), channel_id=1, source_target_pairs={{0,4},{1,5},{2,6},{3,7},{4,0},{5,1},{6,2},{7,3},{8,12},{9,13},{10,... | collective-permute-start | bytes 1769480 | tf_op jit(solution)/shard_map/ppermute | solution.py:14
  66.7 26.2 %copy-start.21 = (f32[768]{0:T(1024)}, f32[768]{0:T(1024)S(1)}, u32[]{:S(2)}) copy-start(f32[768]{0:T(1024)S(1)} %convert_element_type.215) | copy-start | bytes 9220
  69.4 23.5 %copy-start.23 = (f32[1024]{0:T(1024)}, f32[1024]{0:T(1024)S(1)}, u32[]{:S(2)}) copy-start(f32[1024]{0:T(1024)S(1)} %add_rsqrt_fusion.1) | copy-start | bytes 12292
  69.9 13.2 %copy-start.13 = (f32[1024,32]{0,1:T(8,128)}, f32[1024,32]{0,1:T(8,128)S(1)}, u32[]{:S(2)}) copy-start(f32[1024,32]{0,1:T(8,128)S(1)} %get-tuple-element.306) | copy-start | bytes 393220
  69.9 13.2 %copy-start.15 = (f32[1024,32]{0,1:T(8,128)}, f32[1024,32]{0,1:T(8,128)S(1)}, u32[]{:S(2)}) copy-start(f32[1024,32]{0,1:T(8,128)S(1)} %get-tuple-element.307) | copy-start | bytes 393220
  183.6 27.1 %copy-start.7 = (bf16[1,1024,768]{1,2,0:T(8,128)(2,1)S(1)}, bf16[1,1024,768]{1,2,0:T(8,128)(2,1)}, u32[]{:S(2)}) copy-start(bf16[1,1024,768]{1,2,0:T(8,128)(2,1)} %copy.80) | copy-start | bytes 4718596
  210.6 13.2 %copy-start.26 = (bf16[768,2048]{1,0:T(8,128)(2,1)S(1)}, bf16[768,2048]{1,0:T(8,128)(2,1)}, u32[]{:S(2)}) copy-start(bf16[768,2048]{1,0:T(8,128)(2,1)} %all-gather.14.cloned.1.call-done) | copy-start | bytes 9437188
  246.2 206.5 %reduce-scatter.10.cloned.1.call-start = ((), (), s32[]{:S(2)}) async-start(), calls=%async_computation.15 | async-start | bytes 2654208 | tf_op jit(solution)/shard_map/reduce_scatter | solution.py:260
  246.2 149.8 %copy-start.14 = (f32[1024,32]{0,1:T(8,128)S(1)}, f32[1024,32]{0,1:T(8,128)}, u32[]{:S(2)}) copy-start(f32[1024,32]{0,1:T(8,128)} %copy-done.13) | copy-start | bytes 393220
  246.2 149.8 %copy-start.16 = (f32[1024,32]{0,1:T(8,128)S(1)}, f32[1024,32]{0,1:T(8,128)}, u32[]{:S(2)}) copy-start(f32[1024,32]{0,1:T(8,128)} %copy-done.15) | copy-start | bytes 393220
  405.3 74.2 %reduce-scatter.8.cloned.1.call-start = ((), (), s32[]{:S(2)}) async-start(), calls=%async_computation.14 | async-start | bytes 2654208 | tf_op jit(solution)/shard_map/reduce_scatter | solution.py:259
  410.9 106.9 %reduce-scatter.12.cloned.1.call-start = ((), (), s32[]{:S(2)}) async-start(), calls=%async_computation.16 | async-start | bytes 2654208 | tf_op jit(solution)/shard_map/reduce_scatter | solution.py:261
  413.9 174.7 %reduce-scatter.16.cloned.1.call-start = ((), (), s32[]{:S(2)}) async-start(), calls=%async_computation.18 | async-start | bytes 7077888 | tf_op jit(solution)/shard_map/reduce_scatter | solution.py:263
  422.7 236.5 %reduce-scatter.18.cloned.1.call-start = ((), (), s32[]{:S(2)}) async-start(), calls=%async_computation.19 | async-start | bytes 7077888 | tf_op jit(solution)/shard_map/reduce_scatter | solution.py:264
  431.7 297.8 %reduce-scatter.20.cloned.1.call-start = ((), (), s32[]{:S(2)}) async-start(), calls=%async_computation.20 | async-start | bytes 7077888 | tf_op jit(solution)/shard_map/reduce_scatter | solution.py:265
  440.7 356.7 %all-reduce.10.cloned.1.call-start = ((), (), s32[]{:S(2)}) async-start(), calls=%async_computation.21 | async-start | bytes 3538944 | tf_op jit(solution)/shard_map/psum | solution.py:270
  797.4 7.4 copy-start.18
  797.4 8.1 copy-start.17
  (18 other events, 65.7 us)
Sparse Core Ops, SparseCore 0:
  9.6 30.6 all-gather.7
  42.0 28.8 all-gather.9
  72.6 21.2 all-gather.11
  95.4 37.8 all-gather.13
  134.8 37.1 all-gather.15
  173.4 37.1 all-gather.17
  212.2 21.6 all-gather.19
  246.3 35.9 reduce-scatter.13
  405.4 35.9 reduce-scatter.9
  443.5 35.9 reduce-scatter.7
  481.8 35.9 reduce-scatter.11
  519.9 68.6 reduce-scatter.15
  590.9 68.1 reduce-scatter.17
  661.3 68.1 reduce-scatter.19
  734.4 62.8 all-reduce.9
